TPU v7x, 32 devices: a whole 2x2x4 slice. The times are simulated.
32 devices in a mesh: tm: 16 (over z, y, x), rows: 2 (over core).
Axes of the slice: x: 2, y: 2, z: 4, core: 2. Of those that a mesh axis runs over, the one named last changes fastest.
Arguments:
- resid: float32 [2, 16, 16, 512], P(None, 'tm', 'rows'), may hold values from -3 to 3
- basis: float32 [4, 2, 16, 16, 512], P(None, None, 'tm', 'rows'), may hold values from -0.01171875 to 0.01171875
Outputs:
- precond: float32 [2, 16, 16, 512], P(None, 'tm', 'rows')
- image: float32 [2, 16, 16, 512], P(None, 'tm', 'rows')
- gram: float32 [5], replicated
All inputs are finite; a program needn't handle non-finite values.
Results may differ from a plain program's by a relative error of at most 0.0005.
Values sent between devices are 32-bit elements; how exact they have to be, the bound alone decides.
A program may use at most 64 MiB of HBM per device.

v0:
```python
import math
import jax
import jax.numpy as jnp
from jax import lax
from jax.sharding import PartitionSpec as P

SWEEPS = 4
ALPHA = 0.01


def padded_2(shard, sides, width):
    for axis, dim in sides:
        count, length = (lax.axis_size(axis), shard.shape[dim])
        up = [(i, (i + 1) % count) for i in range(count - 1)]
        down = [(j, i) for i, j in up]
        last = lax.slice_in_dim(shard, length - width, length, axis=dim)
        first = lax.slice_in_dim(shard, 0, width, axis=dim)
        before = lax.ppermute(last, axis, up)
        after = lax.ppermute(first, axis, down)
        shard = jnp.concatenate([before, shard, after], axis=dim)
    return shard


def shifted(value, axis, steps):
    count = lax.axis_size(axis)
    first, last = (max(0, -steps), min(count, count - steps))
    return lax.ppermute(value, axis, [(source, source + steps) for source in range(first, last)])


def neighbours(padded):
    middle = padded[:, 1:-1]
    sides = jnp.pad(middle, ((0, 0), (0, 0), (1, 1)))
    return padded[:, 2:] + padded[:, :-2] + sides[:, :, 2:] + sides[:, :, :-2]


def cmul(left, right_re, right_im):
    return jnp.stack(
        [left[0] * right_re - left[1] * right_im, left[0] * right_im + left[1] * right_re]
    )


def phases(first, second, steps):
    turns = first * second % steps
    angle = turns.astype(jnp.float32) * (2.0 * math.pi / steps)
    return (jnp.cos(angle), jnp.sin(angle))


def on_device(resid, basis):
    steps = lax.axis_size("tm")
    coupling = 16.0 / (steps * steps)
    me = lax.axis_index("tm")
    rows_dev = resid.shape[2]
    cols = resid.shape[3]
    cells = rows_dev * cols
    piece = cells // steps
    mine = me.astype(jnp.float32)
    gamma = jnp.power(jnp.float32(ALPHA), mine / steps)
    scaled = resid[:, 0] * gamma
    ordinal = jnp.arange(steps, dtype=jnp.int32)
    cos_table, sin_table = phases(ordinal[:, None], ordinal[None, :], steps)
    blocks = lax.all_to_all(
        scaled.reshape(1, 2, cells), "tm", split_axis=2, concat_axis=0, tiled=True
    )
    flat = blocks.reshape(steps, 2 * piece)
    real_part = jnp.dot(cos_table, flat, precision=lax.Precision.HIGHEST)
    imag_part = -jnp.dot(sin_table, flat, precision=lax.Precision.HIGHEST)
    stacked = jnp.stack([real_part, imag_part], 1).reshape(steps, 2, 2, piece)
    spectrum = lax.all_to_all(stacked, "tm", split_axis=0, concat_axis=3, tiled=True)
    rhat = spectrum[0].reshape(2, 2, rows_dev, cols)
    base = jnp.power(jnp.float32(ALPHA), jnp.float32(1.0) / steps)
    angle = mine * (2.0 * math.pi / steps)
    lam_re = 1.0 - base * jnp.cos(angle)
    lam_im = base * jnp.sin(angle)
    disp_spec = rhat[:, 0]
    right = cmul(disp_spec, lam_re, lam_im) + rhat[:, 1]
    den_re = lam_re * lam_re - lam_im * lam_im + 4.0 * coupling
    den_im = 2.0 * lam_re * lam_im
    magnitude = den_re * den_re + den_im * den_im
    inv_re = den_re / magnitude
    inv_im = -den_im / magnitude
    uhat = cmul(right, inv_re, inv_im)
    for sweep in range(SWEEPS - 1):
        padded = padded_2(uhat, (("rows", 1),), 1)
        uhat = cmul(right + coupling * neighbours(padded), inv_re, inv_im)
    vhat = cmul(uhat, lam_re, lam_im) - disp_spec
    yhat = jnp.stack([uhat, vhat], 1)
    spread = lax.all_to_all(
        yhat.reshape(1, 2, 2, cells), "tm", split_axis=3, concat_axis=0, tiled=True
    )
    real_rows = spread[:, 0].reshape(steps, 2 * piece)
    imag_rows = spread[:, 1].reshape(steps, 2 * piece)
    undo = jnp.power(jnp.float32(ALPHA), -ordinal.astype(jnp.float32) / steps) / steps
    history = jnp.dot(cos_table, real_rows, precision=lax.Precision.HIGHEST) - jnp.dot(
        sin_table, imag_rows, precision=lax.Precision.HIGHEST
    )
    history = (history * undo[:, None]).reshape(steps, 2, piece)
    returned = lax.all_to_all(history, "tm", split_axis=0, concat_axis=2, tiled=True)
    precond = returned[0].reshape(2, rows_dev, cols)
    earlier = shifted(precond, "tm", 1)
    disp_rim = padded_2(precond[0:1], (("rows", 1),), 1)
    laplace = neighbours(disp_rim)[0] - 4.0 * precond[0]
    first = precond[0] - earlier[0] - precond[1]
    second = precond[1] - earlier[1] - coupling * laplace
    image = jnp.stack([first, second])
    inner = jnp.sum(basis[:, :, 0] * image[None], axis=(1, 2, 3))
    count = 2.0 * steps * rows_dev * lax.axis_size("rows") * cols
    squares = jnp.sum(image * image) / count
    local_terms = jnp.concatenate([inner, squares[None]])
    gram = lax.psum(local_terms, ("tm", "rows"))
    return (precond[:, None], image[:, None], gram)


def solution(mesh):
    in_specs = (P(None, "tm", "rows", None), P(None, None, "tm", "rows", None))
    out_specs = (P(None, "tm", "rows", None), P(None, "tm", "rows", None), P())
    return jax.shard_map(
        on_device, mesh=mesh, in_specs=in_specs, out_specs=out_specs, check_vma=False
    )
```

profile of v0, /device:TPU:0, one launch (start us, length us, event | category | flops | bytes accessed | tf_op | source)
XLA Modules:
  0.0 169.4 jit_solution(10434036143663607024)
XLA Ops:
  2.6 19.4 %reduce.4 = f32[4096,2]{1,0:T(8,128)} reduce(f32[4096,1,2]{2,1,0:T(1,128)S(1)} %bitcast.83, f32[]{:T(128)} %broadcast.139), dimensions={1}, to_apply=%bitcast.65.reduce_sub_computation | reduce | bytes 65540
  22.0 3.0 %reshape.138 = f32[16,1,512]{2,1,0:T(1,128)S(1)} reshape(f32[4096,2]{1,0:T(8,128)} %reduce.4) | data formatting | bytes 65536
  25.0 15.5 %all_to_all.63 = f32[16,1,512]{2,1,0:T(1,128)S(1)} all-to-all(f32[16,1,512]{2,1,0:T(1,128)S(1)} %reshape.138), channel_id=1, replica_groups=mesh['tm'=16,'rows'=2] {'tm'}, dimensions={0} | all-to-all | bytes 65536 | tf_op jit(solution)/shard_map/all_to_all | solution.py:61
  41.3 3.4 %reshape.139 = f32[4096,1,2]{2,1,0:T(1,128)S(1)} reshape(f32[16,512]{1,0:T(8,128)S(1)} %reduce.5) | data formatting | bytes 65536
  46.5 3.5 %all-to-all-start.1 = ((f32[16,2,2,256]{3,2,1,0:T(2,128)}), f32[16,2,2,256]{3,2,1,0:T(2,128)S(1)}, u32[]{:S(2)}, u32[]{:S(2)}) async-start(f32[16,2,2,256]{3,2,1,0:T(2,128)} %copy.48), calls=%async_computation.1 | async-start | bytes 131072 | tf_op jit(solution)/shard_map/all_to_all | solution.py:68
  50.2 7.2 %all-to-all-done.1 = f32[16,2,2,256]{3,2,1,0:T(2,128)S(1)} async-done(((f32[16,2,2,256]{3,2,1,0:T(2,128)}), f32[16,2,2,256]{3,2,1,0:T(2,128)S(1)}, u32[]{:S(2)}, u32[]{:S(2)}) %all-to-all-start.1) | async-done | bytes 65568 | tf_op jit(solution)/shard_map/all_to_all | solution.py:68
  57.6 1.3 collective-permute-start
  58.9 3.0 %collective-permute-start.1 = (f32[2,1,512]{2,1,0:T(1,128)S(1)}, f32[2,1,512]{2,1,0:T(1,128)S(1)}, u32[]{:S(2)}, u32[]{:S(2)}) collective-permute-start(f32[2,1,512]{2,1,0:T(1,128)S(1)} %get-tuple-element.26), channel_id=1, source_target_pairs={{0,1},{2,3},{4,5},{6,7},{8,9},{10,11},{12,13},{14,15},{16,17},{18,... | collective-permute-start | bytes 12296 | tf_op jit(solution)/shard_map/ppermute | solution.py:18
  62.9 1.3 collective-permute-start.2
  64.2 3.0 %collective-permute-start.3 = (f32[2,1,512]{2,1,0:T(1,128)S(1)}, f32[2,1,512]{2,1,0:T(1,128)S(1)}, u32[]{:S(2)}, u32[]{:S(2)}) collective-permute-start(f32[2,1,512]{2,1,0:T(1,128)S(1)} %get-tuple-element.22), channel_id=1, source_target_pairs={{0,1},{2,3},{4,5},{6,7},{8,9},{10,11},{12,13},{14,15},{16,17},{18,... | collective-permute-start | bytes 12296 | tf_op jit(solution)/shard_map/ppermute | solution.py:18
  68.1 1.3 collective-permute-start.4
  69.4 3.2 %collective-permute-start.5 = (f32[2,1,512]{2,1,0:T(1,128)S(1)}, f32[2,1,512]{2,1,0:T(1,128)S(1)}, u32[]{:S(2)}, u32[]{:S(2)}) collective-permute-start(f32[2,1,512]{2,1,0:T(1,128)S(1)} %get-tuple-element.18), channel_id=1, source_target_pairs={{0,1},{2,3},{4,5},{6,7},{8,9},{10,11},{12,13},{14,15},{16,17},{18,... | collective-permute-start | bytes 12296 | tf_op jit(solution)/shard_map/ppermute | solution.py:18
  73.5 4.4 %copy.51 = f32[1,2,2,4096]{2,1,0,3:T(2,128)} copy(f32[1,2,2,4096]{3,1,2,0:T(2,128)S(1)} %pad_maximum_fusion.1) | data formatting | bytes 131072 | tf_op jit(solution)/shard_map/stack | solution.py:86
  77.9 8.1 %reshape.140 = f32[16,1,1024]{2,1,0:T(1,128)} reshape(f32[4096,1,2,2]{3,2,1,0:T(2,128)} %bitcast.81) | data formatting | bytes 131072
  86.0 3.5 %all-to-all-start.2 = ((f32[16,1,1024]{2,1,0:T(1,128)}), f32[16,1,1024]{2,1,0:T(1,128)S(1)}, u32[]{:S(2)}, u32[]{:S(2)}) async-start(f32[16,1,1024]{2,1,0:T(1,128)} %reshape.140), calls=%async_computation.2 | async-start | bytes 131072 | tf_op jit(solution)/shard_map/all_to_all | solution.py:87
  89.5 7.5 %all-to-all-done.2 = f32[16,1,1024]{2,1,0:T(1,128)S(1)} async-done(((f32[16,1,1024]{2,1,0:T(1,128)}), f32[16,1,1024]{2,1,0:T(1,128)S(1)}, u32[]{:S(2)}, u32[]{:S(2)}) %all-to-all-start.2) | async-done | bytes 65568 | tf_op jit(solution)/shard_map/all_to_all | solution.py:87
  97.8 7.7 %reshape.141 = f32[4096,1,2,2]{3,2,1,0:T(2,128)} reshape(f32[16,1024]{1,0:T(8,128)S(1)} %reduce.6) | data formatting | bytes 131072
  105.6 3.6 %copy.57 = f32[1,2,2,16,256]{4,3,2,1,0:T(8,128)S(1)} copy(f32[1,2,2,16,256]{2,1,4,3,0:T(2,128)} %bitcast.82) | data formatting | bytes 131072 | tf_op jit(solution)/shard_map/all_to_all | solution.py:87
  109.7 10.0 %all_to_all.64 = f32[16,2,256]{2,1,0:T(2,128)S(1)} all-to-all(f32[16,2,256]{2,1,0:T(2,128)S(1)} %reshape.134), channel_id=1, replica_groups=mesh['tm'=16,'rows'=2] {'tm'}, dimensions={0} | all-to-all | bytes 65536 | tf_op jit(solution)/shard_map/all_to_all | solution.py:97
  119.8 2.6 %collective-permute-start.6 = (f32[2,8,512]{2,1,0:T(8,128)S(1)}, f32[2,8,512]{2,1,0:T(8,128)S(1)}, u32[]{:S(2)}, u32[]{:S(2)}) collective-permute-start(f32[2,8,512]{2,1,0:T(8,128)S(1)} %reshape_squeeze.15), channel_id=1, source_target_pairs={{0,2},{2,4},{4,6},{6,8},{8,10},{10,12},{12,14},{14,16},{16,18},{18... | collective-permute-start | bytes 98312 | tf_op jit(solution)/shard_map/ppermute | solution.py:27
  122.4 1.3 collective-permute-start.7
  123.7 3.0 %collective-permute-start.8 = (f32[1,1,512]{2,1,0:T(1,128)S(1)}, f32[1,1,512]{2,1,0:T(1,128)S(1)}, u32[]{:S(2)}, u32[]{:S(2)}) collective-permute-start(f32[1,1,512]{2,1,0:T(1,128)S(1)} %get-tuple-element.30), channel_id=1, source_target_pairs={{0,1},{2,3},{4,5},{6,7},{8,9},{10,11},{12,13},{14,15},{16,17},{18,... | collective-permute-start | bytes 6152 | tf_op jit(solution)/shard_map/ppermute | solution.py:18
  127.7 1.2 pad_maximum_fusion.18
  130.4 39.0 %psum.7 = f32[5]{0:T(128)} all-reduce(f32[5]{0:T(128)S(1)} %pad_maximum_fusion.21), channel_id=1, replica_groups=mesh['tm'=16,'rows'=2] {'tm','rows'}, use_global_device_ids=true, to_apply=%region_2.3 | all-reduce | flops 5 | bytes 40 | tf_op jit(solution)/shard_map/psum | solution.py:109
  (66 shorter events, 10.2 us)
Async XLA Ops:
  46.5 11.0 %all-to-all-start.1 = ((f32[16,2,2,256]{3,2,1,0:T(2,128)}), f32[16,2,2,256]{3,2,1,0:T(2,128)S(1)}, u32[]{:S(2)}, u32[]{:S(2)}) async-start(f32[16,2,2,256]{3,2,1,0:T(2,128)} %copy.48), calls=%async_computation.1 | async-start | bytes 131072 | tf_op jit(solution)/shard_map/all_to_all | solution.py:68
  57.6 4.3 %collective-permute-start = (f32[2,1,512]{2,1,0:T(1,128)S(1)}, f32[2,1,512]{2,1,0:T(1,128)S(1)}, u32[]{:S(2)}, u32[]{:S(2)}) collective-permute-start(f32[2,1,512]{2,1,0:T(1,128)S(1)} %get-tuple-element.25), channel_id=1, source_target_pairs={{1,0},{3,2},{5,4},{7,6},{9,8},{11,10},{13,12},{15,14},{17,16},{19,... | collective-permute-start | bytes 12296 | tf_op jit(solution)/shard_map/ppermute | solution.py:19
  58.9 3.8 %collective-permute-start.1 = (f32[2,1,512]{2,1,0:T(1,128)S(1)}, f32[2,1,512]{2,1,0:T(1,128)S(1)}, u32[]{:S(2)}, u32[]{:S(2)}) collective-permute-start(f32[2,1,512]{2,1,0:T(1,128)S(1)} %get-tuple-element.26), channel_id=1, source_target_pairs={{0,1},{2,3},{4,5},{6,7},{8,9},{10,11},{12,13},{14,15},{16,17},{18,... | collective-permute-start | bytes 12296 | tf_op jit(solution)/shard_map/ppermute | solution.py:18
  62.9 4.3 %collective-permute-start.2 = (f32[2,1,512]{2,1,0:T(1,128)S(1)}, f32[2,1,512]{2,1,0:T(1,128)S(1)}, u32[]{:S(2)}, u32[]{:S(2)}) collective-permute-start(f32[2,1,512]{2,1,0:T(1,128)S(1)} %get-tuple-element.21), channel_id=1, source_target_pairs={{1,0},{3,2},{5,4},{7,6},{9,8},{11,10},{13,12},{15,14},{17,16},{19,... | collective-permute-start | bytes 12296 | tf_op jit(solution)/shard_map/ppermute | solution.py:19
  64.2 3.8 %collective-permute-start.3 = (f32[2,1,512]{2,1,0:T(1,128)S(1)}, f32[2,1,512]{2,1,0:T(1,128)S(1)}, u32[]{:S(2)}, u32[]{:S(2)}) collective-permute-start(f32[2,1,512]{2,1,0:T(1,128)S(1)} %get-tuple-element.22), channel_id=1, source_target_pairs={{0,1},{2,3},{4,5},{6,7},{8,9},{10,11},{12,13},{14,15},{16,17},{18,... | collective-permute-start | bytes 12296 | tf_op jit(solution)/shard_map/ppermute | solution.py:18
  68.1 4.5 %collective-permute-start.4 = (f32[2,1,512]{2,1,0:T(1,128)S(1)}, f32[2,1,512]{2,1,0:T(1,128)S(1)}, u32[]{:S(2)}, u32[]{:S(2)}) collective-permute-start(f32[2,1,512]{2,1,0:T(1,128)S(1)} %get-tuple-element.17), channel_id=1, source_target_pairs={{1,0},{3,2},{5,4},{7,6},{9,8},{11,10},{13,12},{15,14},{17,16},{19,... | collective-permute-start | bytes 12296 | tf_op jit(solution)/shard_map/ppermute | solution.py:19
  69.4 3.8 %collective-permute-start.5 = (f32[2,1,512]{2,1,0:T(1,128)S(1)}, f32[2,1,512]{2,1,0:T(1,128)S(1)}, u32[]{:S(2)}, u32[]{:S(2)}) collective-permute-start(f32[2,1,512]{2,1,0:T(1,128)S(1)} %get-tuple-element.18), channel_id=1, source_target_pairs={{0,1},{2,3},{4,5},{6,7},{8,9},{10,11},{12,13},{14,15},{16,17},{18,... | collective-permute-start | bytes 12296 | tf_op jit(solution)/shard_map/ppermute | solution.py:18
  86.0 11.0 %all-to-all-start.2 = ((f32[16,1,1024]{2,1,0:T(1,128)}), f32[16,1,1024]{2,1,0:T(1,128)S(1)}, u32[]{:S(2)}, u32[]{:S(2)}) async-start(f32[16,1,1024]{2,1,0:T(1,128)} %reshape.140), calls=%async_computation.2 | async-start | bytes 131072 | tf_op jit(solution)/shard_map/all_to_all | solution.py:87
  105.6 24.0 %copy-start = (f32[4,2,1,8,512]{4,3,2,1,0:T(8,128)S(1)}, f32[4,2,1,8,512]{4,3,2,1,0:T(8,128)}, u32[]{:S(2)}) copy-start(f32[4,2,1,8,512]{4,3,2,1,0:T(8,128)} %param.3) | copy-start | bytes 393220
  119.8 7.8 %collective-permute-start.6 = (f32[2,8,512]{2,1,0:T(8,128)S(1)}, f32[2,8,512]{2,1,0:T(8,128)S(1)}, u32[]{:S(2)}, u32[]{:S(2)}) collective-permute-start(f32[2,8,512]{2,1,0:T(8,128)S(1)} %reshape_squeeze.15), channel_id=1, source_target_pairs={{0,2},{2,4},{4,6},{6,8},{8,10},{10,12},{12,14},{14,16},{16,18},{18... | collective-permute-start | bytes 98312 | tf_op jit(solution)/shard_map/ppermute | solution.py:27
  122.4 4.4 %collective-permute-start.7 = (f32[1,1,512]{2,1,0:T(1,128)S(1)}, f32[1,1,512]{2,1,0:T(1,128)S(1)}, u32[]{:S(2)}, u32[]{:S(2)}) collective-permute-start(f32[1,1,512]{2,1,0:T(1,128)S(1)} %get-tuple-element.29), channel_id=1, source_target_pairs={{1,0},{3,2},{5,4},{7,6},{9,8},{11,10},{13,12},{15,14},{17,16},{19,... | collective-permute-start | bytes 6152 | tf_op jit(solution)/shard_map/ppermute | solution.py:19
  123.7 3.8 %collective-permute-start.8 = (f32[1,1,512]{2,1,0:T(1,128)S(1)}, f32[1,1,512]{2,1,0:T(1,128)S(1)}, u32[]{:S(2)}, u32[]{:S(2)}) collective-permute-start(f32[1,1,512]{2,1,0:T(1,128)S(1)} %get-tuple-element.30), channel_id=1, source_target_pairs={{0,1},{2,3},{4,5},{6,7},{8,9},{10,11},{12,13},{14,15},{16,17},{18,... | collective-permute-start | bytes 6152 | tf_op jit(solution)/shard_map/ppermute | solution.py:18
where the time goes:
time: 170 us; the launch traced here: 169 us
  blocking collectives  64.5 us (38%)
  local copies, waits for them, and re-layouts  33.7 us (20%)
  starting transfers between devices  27 us (16%)
  other arithmetic  23.6 us (14%)
  waiting for transfers between devices  17.7 us (10%)
  between operations  2.06 us (1%)
    psum x1, blocking collectives, on_device(): gram = lax.psum(local_terms, ('tm', 'rows'))  39 us
    unnamed x10, local copies, waits for them, and re-layouts  22.8 us
    unnamed x1, other arithmetic  19.4 us
    all_to_all x1, blocking collectives, on_device(): lax.all_to_all(scaled.reshape(1, 2, cells), 'tm', split_axis=2, concat_ax...  15.5 us
    ppermute x4, starting transfers between devices, padded_2(): before = lax.ppermute(last, axis, up)  12.3 us
    all_to_all x1, blocking collectives, on_device(): lax.all_to_all(history, 'tm', split_axis=0, concat_axis=2, tiled=True)  9.98 us
    all_to_all x1, waiting for transfers between devices, on_device(): lax.all_to_all(yhat.reshape(1, 2, 2, cells), 'tm', split_axis=3, concat_a...  7.49 us
    all_to_all x1, waiting for transfers between devices, on_device(): lax.all_to_all(stacked, 'tm', split_axis=0, concat_axis=3, tiled=True)  7.25 us
  transfers between devices with their start and end apart: 11, of which 6 were waited for; matrix products, arithmetic and copies ran while one was open for 0% of the time, Pallas kernels for 0%

commit v1 on v0

--- a/solution.py
+++ b/solution.py
@@ -106,7 +106,9 @@
     count = 2.0 * steps * rows_dev * lax.axis_size("rows") * cols
     squares = jnp.sum(image * image) / count
     local_terms = jnp.concatenate([inner, squares[None]])
-    gram = lax.psum(local_terms, ("tm", "rows"))
+    gram = local_terms
+    for kk in ("rows", "tm"):
+        gram = jax.lax.psum(gram, kk)
     return (precond[:, None], image[:, None], gram)
 
 

time: 170 us -> 172 us (1.012)
  blocking collectives: 64.5 us -> 66.4 us
    psum x1 -> x2, blocking collectives: 39 us -> 40.9 us  [on_device(): gram = jax.lax.psum(gram, kk)]
where the time goes in v1:
time: 172 us; the launch traced here: 171 us
  blocking collectives  66.4 us (39%)
  local copies, waits for them, and re-layouts  33.7 us (20%)
  starting transfers between devices  27 us (16%)
  other arithmetic  23.6 us (14%)
  waiting for transfers between devices  17.7 us (10%)
  between operations  2.02 us (1%)
    psum x2, blocking collectives, on_device(): gram = jax.lax.psum(gram, kk)  40.9 us
    unnamed x10, local copies, waits for them, and re-layouts  22.8 us
    unnamed x1, other arithmetic  19.4 us
    all_to_all x1, blocking collectives, on_device(): lax.all_to_all(scaled.reshape(1, 2, cells), 'tm', split_axis=2, concat_ax...  15.5 us
    ppermute x4, starting transfers between devices, padded_2(): before = lax.ppermute(last, axis, up)  12.3 us
    all_to_all x1, blocking collectives, on_device(): lax.all_to_all(history, 'tm', split_axis=0, concat_axis=2, tiled=True)  9.98 us
    all_to_all x1, waiting for transfers between devices, on_device(): lax.all_to_all(yhat.reshape(1, 2, 2, cells), 'tm', split_axis=3, concat_a...  7.49 us
    all_to_all x1, waiting for transfers between devices, on_device(): lax.all_to_all(stacked, 'tm', split_axis=0, concat_axis=3, tiled=True)  7.25 us
  transfers between devices with their start and end apart: 11, of which 6 were waited for; matrix products, arithmetic and copies ran while one was open for 0% of the time, Pallas kernels for 0%

profile of v1, /device:TPU:0, one launch (start us, length us, event | category | flops | bytes accessed | tf_op | source)
XLA Modules:
  0.0 171.3 jit_solution(7038172421289063082)
XLA Ops:
  2.6 19.4 %reduce.4 = f32[4096,2]{1,0:T(8,128)} reduce(f32[4096,1,2]{2,1,0:T(1,128)S(1)} %bitcast.83, f32[]{:T(128)} %broadcast.139), dimensions={1}, to_apply=%bitcast.65.reduce_sub_computation | reduce | bytes 65540
  22.0 3.0 %reshape.138 = f32[16,1,512]{2,1,0:T(1,128)S(1)} reshape(f32[4096,2]{1,0:T(8,128)} %reduce.4) | data formatting | bytes 65536
  25.0 15.5 %all_to_all.63 = f32[16,1,512]{2,1,0:T(1,128)S(1)} all-to-all(f32[16,1,512]{2,1,0:T(1,128)S(1)} %reshape.138), channel_id=1, replica_groups=mesh['tm'=16,'rows'=2] {'tm'}, dimensions={0} | all-to-all | bytes 65536 | tf_op jit(solution)/shard_map/all_to_all | solution.py:61
  41.3 3.4 %reshape.139 = f32[4096,1,2]{2,1,0:T(1,128)S(1)} reshape(f32[16,512]{1,0:T(8,128)S(1)} %reduce.5) | data formatting | bytes 65536
  46.5 3.5 %all-to-all-start.1 = ((f32[16,2,2,256]{3,2,1,0:T(2,128)}), f32[16,2,2,256]{3,2,1,0:T(2,128)S(1)}, u32[]{:S(2)}, u32[]{:S(2)}) async-start(f32[16,2,2,256]{3,2,1,0:T(2,128)} %copy.48), calls=%async_computation.1 | async-start | bytes 131072 | tf_op jit(solution)/shard_map/all_to_all | solution.py:68
  50.3 7.2 %all-to-all-done.1 = f32[16,2,2,256]{3,2,1,0:T(2,128)S(1)} async-done(((f32[16,2,2,256]{3,2,1,0:T(2,128)}), f32[16,2,2,256]{3,2,1,0:T(2,128)S(1)}, u32[]{:S(2)}, u32[]{:S(2)}) %all-to-all-start.1) | async-done | bytes 65568 | tf_op jit(solution)/shard_map/all_to_all | solution.py:68
  57.6 1.3 collective-permute-start
  58.9 3.0 %collective-permute-start.1 = (f32[2,1,512]{2,1,0:T(1,128)S(1)}, f32[2,1,512]{2,1,0:T(1,128)S(1)}, u32[]{:S(2)}, u32[]{:S(2)}) collective-permute-start(f32[2,1,512]{2,1,0:T(1,128)S(1)} %get-tuple-element.26), channel_id=1, source_target_pairs={{0,1},{2,3},{4,5},{6,7},{8,9},{10,11},{12,13},{14,15},{16,17},{18,... | collective-permute-start | bytes 12296 | tf_op jit(solution)/shard_map/ppermute | solution.py:18
  62.9 1.3 collective-permute-start.2
  64.2 3.0 %collective-permute-start.3 = (f32[2,1,512]{2,1,0:T(1,128)S(1)}, f32[2,1,512]{2,1,0:T(1,128)S(1)}, u32[]{:S(2)}, u32[]{:S(2)}) collective-permute-start(f32[2,1,512]{2,1,0:T(1,128)S(1)} %get-tuple-element.22), channel_id=1, source_target_pairs={{0,1},{2,3},{4,5},{6,7},{8,9},{10,11},{12,13},{14,15},{16,17},{18,... | collective-permute-start | bytes 12296 | tf_op jit(solution)/shard_map/ppermute | solution.py:18
  68.1 1.3 collective-permute-start.4
  69.4 3.2 %collective-permute-start.5 = (f32[2,1,512]{2,1,0:T(1,128)S(1)}, f32[2,1,512]{2,1,0:T(1,128)S(1)}, u32[]{:S(2)}, u32[]{:S(2)}) collective-permute-start(f32[2,1,512]{2,1,0:T(1,128)S(1)} %get-tuple-element.18), channel_id=1, source_target_pairs={{0,1},{2,3},{4,5},{6,7},{8,9},{10,11},{12,13},{14,15},{16,17},{18,... | collective-permute-start | bytes 12296 | tf_op jit(solution)/shard_map/ppermute | solution.py:18
  73.5 4.4 %copy.51 = f32[1,2,2,4096]{2,1,0,3:T(2,128)} copy(f32[1,2,2,4096]{3,1,2,0:T(2,128)S(1)} %pad_maximum_fusion.1) | data formatting | bytes 131072 | tf_op jit(solution)/shard_map/stack | solution.py:86
  77.9 8.1 %reshape.140 = f32[16,1,1024]{2,1,0:T(1,128)} reshape(f32[4096,1,2,2]{3,2,1,0:T(2,128)} %bitcast.81) | data formatting | bytes 131072
  86.0 3.5 %all-to-all-start.2 = ((f32[16,1,1024]{2,1,0:T(1,128)}), f32[16,1,1024]{2,1,0:T(1,128)S(1)}, u32[]{:S(2)}, u32[]{:S(2)}) async-start(f32[16,1,1024]{2,1,0:T(1,128)} %reshape.140), calls=%async_computation.2 | async-start | bytes 131072 | tf_op jit(solution)/shard_map/all_to_all | solution.py:87
  89.5 7.5 %all-to-all-done.2 = f32[16,1,1024]{2,1,0:T(1,128)S(1)} async-done(((f32[16,1,1024]{2,1,0:T(1,128)}), f32[16,1,1024]{2,1,0:T(1,128)S(1)}, u32[]{:S(2)}, u32[]{:S(2)}) %all-to-all-start.2) | async-done | bytes 65568 | tf_op jit(solution)/shard_map/all_to_all | solution.py:87
  97.8 7.7 %reshape.141 = f32[4096,1,2,2]{3,2,1,0:T(2,128)} reshape(f32[16,1024]{1,0:T(8,128)S(1)} %reduce.6) | data formatting | bytes 131072
  105.6 3.6 %copy.57 = f32[1,2,2,16,256]{4,3,2,1,0:T(8,128)S(1)} copy(f32[1,2,2,16,256]{2,1,4,3,0:T(2,128)} %bitcast.82) | data formatting | bytes 131072 | tf_op jit(solution)/shard_map/all_to_all | solution.py:87
  109.7 10.0 %all_to_all.64 = f32[16,2,256]{2,1,0:T(2,128)S(1)} all-to-all(f32[16,2,256]{2,1,0:T(2,128)S(1)} %reshape.134), channel_id=1, replica_groups=mesh['tm'=16,'rows'=2] {'tm'}, dimensions={0} | all-to-all | bytes 65536 | tf_op jit(solution)/shard_map/all_to_all | solution.py:97
  119.8 2.6 %collective-permute-start.6 = (f32[2,8,512]{2,1,0:T(8,128)S(1)}, f32[2,8,512]{2,1,0:T(8,128)S(1)}, u32[]{:S(2)}, u32[]{:S(2)}) collective-permute-start(f32[2,8,512]{2,1,0:T(8,128)S(1)} %reshape_squeeze.15), channel_id=1, source_target_pairs={{0,2},{2,4},{4,6},{6,8},{8,10},{10,12},{12,14},{14,16},{16,18},{18... | collective-permute-start | bytes 98312 | tf_op jit(solution)/shard_map/ppermute | solution.py:27
  122.5 1.3 collective-permute-start.7
  123.8 3.0 %collective-permute-start.8 = (f32[1,1,512]{2,1,0:T(1,128)S(1)}, f32[1,1,512]{2,1,0:T(1,128)S(1)}, u32[]{:S(2)}, u32[]{:S(2)}) collective-permute-start(f32[1,1,512]{2,1,0:T(1,128)S(1)} %get-tuple-element.30), channel_id=1, source_target_pairs={{0,1},{2,3},{4,5},{6,7},{8,9},{10,11},{12,13},{14,15},{16,17},{18,... | collective-permute-start | bytes 6152 | tf_op jit(solution)/shard_map/ppermute | solution.py:18
  129.8 2.5 %psum.14 = f32[5]{0:T(128)S(1)} all-reduce(f32[5]{0:T(128)S(1)} %pad_maximum_fusion.21), channel_id=1, replica_groups=mesh['tm'=16,'rows'=2] {'rows'}, use_global_device_ids=true, to_apply=%region_2.3 | all-reduce | flops 5 | bytes 40 | tf_op jit(solution)/shard_map/psum | solution.py:111
  132.8 38.4 %psum.15 = f32[5]{0:T(128)} all-reduce(f32[5]{0:T(128)S(1)} %psum.14), channel_id=1, replica_groups=mesh['tm'=16,'rows'=2] {'tm'}, use_global_device_ids=true, to_apply=%region_3.4 | all-reduce | flops 5 | bytes 40 | tf_op jit(solution)/shard_map/psum | solution.py:111
  (67 shorter events, 11.5 us)
Async XLA Ops:
  46.5 11.0 %all-to-all-start.1 = ((f32[16,2,2,256]{3,2,1,0:T(2,128)}), f32[16,2,2,256]{3,2,1,0:T(2,128)S(1)}, u32[]{:S(2)}, u32[]{:S(2)}) async-start(f32[16,2,2,256]{3,2,1,0:T(2,128)} %copy.48), calls=%async_computation.1 | async-start | bytes 131072 | tf_op jit(solution)/shard_map/all_to_all | solution.py:68
  57.6 4.3 %collective-permute-start = (f32[2,1,512]{2,1,0:T(1,128)S(1)}, f32[2,1,512]{2,1,0:T(1,128)S(1)}, u32[]{:S(2)}, u32[]{:S(2)}) collective-permute-start(f32[2,1,512]{2,1,0:T(1,128)S(1)} %get-tuple-element.25), channel_id=1, source_target_pairs={{1,0},{3,2},{5,4},{7,6},{9,8},{11,10},{13,12},{15,14},{17,16},{19,... | collective-permute-start | bytes 12296 | tf_op jit(solution)/shard_map/ppermute | solution.py:19
  58.9 3.8 %collective-permute-start.1 = (f32[2,1,512]{2,1,0:T(1,128)S(1)}, f32[2,1,512]{2,1,0:T(1,128)S(1)}, u32[]{:S(2)}, u32[]{:S(2)}) collective-permute-start(f32[2,1,512]{2,1,0:T(1,128)S(1)} %get-tuple-element.26), channel_id=1, source_target_pairs={{0,1},{2,3},{4,5},{6,7},{8,9},{10,11},{12,13},{14,15},{16,17},{18,... | collective-permute-start | bytes 12296 | tf_op jit(solution)/shard_map/ppermute | solution.py:18
  62.9 4.3 %collective-permute-start.2 = (f32[2,1,512]{2,1,0:T(1,128)S(1)}, f32[2,1,512]{2,1,0:T(1,128)S(1)}, u32[]{:S(2)}, u32[]{:S(2)}) collective-permute-start(f32[2,1,512]{2,1,0:T(1,128)S(1)} %get-tuple-element.21), channel_id=1, source_target_pairs={{1,0},{3,2},{5,4},{7,6},{9,8},{11,10},{13,12},{15,14},{17,16},{19,... | collective-permute-start | bytes 12296 | tf_op jit(solution)/shard_map/ppermute | solution.py:19
  64.2 3.8 %collective-permute-start.3 = (f32[2,1,512]{2,1,0:T(1,128)S(1)}, f32[2,1,512]{2,1,0:T(1,128)S(1)}, u32[]{:S(2)}, u32[]{:S(2)}) collective-permute-start(f32[2,1,512]{2,1,0:T(1,128)S(1)} %get-tuple-element.22), channel_id=1, source_target_pairs={{0,1},{2,3},{4,5},{6,7},{8,9},{10,11},{12,13},{14,15},{16,17},{18,... | collective-permute-start | bytes 12296 | tf_op jit(solution)/shard_map/ppermute | solution.py:18
  68.1 4.5 %collective-permute-start.4 = (f32[2,1,512]{2,1,0:T(1,128)S(1)}, f32[2,1,512]{2,1,0:T(1,128)S(1)}, u32[]{:S(2)}, u32[]{:S(2)}) collective-permute-start(f32[2,1,512]{2,1,0:T(1,128)S(1)} %get-tuple-element.17), channel_id=1, source_target_pairs={{1,0},{3,2},{5,4},{7,6},{9,8},{11,10},{13,12},{15,14},{17,16},{19,... | collective-permute-start | bytes 12296 | tf_op jit(solution)/shard_map/ppermute | solution.py:19
  69.4 3.8 %collective-permute-start.5 = (f32[2,1,512]{2,1,0:T(1,128)S(1)}, f32[2,1,512]{2,1,0:T(1,128)S(1)}, u32[]{:S(2)}, u32[]{:S(2)}) collective-permute-start(f32[2,1,512]{2,1,0:T(1,128)S(1)} %get-tuple-element.18), channel_id=1, source_target_pairs={{0,1},{2,3},{4,5},{6,7},{8,9},{10,11},{12,13},{14,15},{16,17},{18,... | collective-permute-start | bytes 12296 | tf_op jit(solution)/shard_map/ppermute | solution.py:18
  86.0 11.0 %all-to-all-start.2 = ((f32[16,1,1024]{2,1,0:T(1,128)}), f32[16,1,1024]{2,1,0:T(1,128)S(1)}, u32[]{:S(2)}, u32[]{:S(2)}) async-start(f32[16,1,1024]{2,1,0:T(1,128)} %reshape.140), calls=%async_computation.2 | async-start | bytes 131072 | tf_op jit(solution)/shard_map/all_to_all | solution.py:87
  105.6 24.0 %copy-start = (f32[4,2,1,8,512]{4,3,2,1,0:T(8,128)S(1)}, f32[4,2,1,8,512]{4,3,2,1,0:T(8,128)}, u32[]{:S(2)}) copy-start(f32[4,2,1,8,512]{4,3,2,1,0:T(8,128)} %param.3) | copy-start | bytes 393220
  119.8 7.8 %collective-permute-start.6 = (f32[2,8,512]{2,1,0:T(8,128)S(1)}, f32[2,8,512]{2,1,0:T(8,128)S(1)}, u32[]{:S(2)}, u32[]{:S(2)}) collective-permute-start(f32[2,8,512]{2,1,0:T(8,128)S(1)} %reshape_squeeze.15), channel_id=1, source_target_pairs={{0,2},{2,4},{4,6},{6,8},{8,10},{10,12},{12,14},{14,16},{16,18},{18... | collective-permute-start | bytes 98312 | tf_op jit(solution)/shard_map/ppermute | solution.py:27
  122.5 4.4 %collective-permute-start.7 = (f32[1,1,512]{2,1,0:T(1,128)S(1)}, f32[1,1,512]{2,1,0:T(1,128)S(1)}, u32[]{:S(2)}, u32[]{:S(2)}) collective-permute-start(f32[1,1,512]{2,1,0:T(1,128)S(1)} %get-tuple-element.29), channel_id=1, source_target_pairs={{1,0},{3,2},{5,4},{7,6},{9,8},{11,10},{13,12},{15,14},{17,16},{19,... | collective-permute-start | bytes 6152 | tf_op jit(solution)/shard_map/ppermute | solution.py:19
  123.8 3.8 %collective-permute-start.8 = (f32[1,1,512]{2,1,0:T(1,128)S(1)}, f32[1,1,512]{2,1,0:T(1,128)S(1)}, u32[]{:S(2)}, u32[]{:S(2)}) collective-permute-start(f32[1,1,512]{2,1,0:T(1,128)S(1)} %get-tuple-element.30), channel_id=1, source_target_pairs={{0,1},{2,3},{4,5},{6,7},{8,9},{10,11},{12,13},{14,15},{16,17},{18,... | collective-permute-start | bytes 6152 | tf_op jit(solution)/shard_map/ppermute | solution.py:18
